TPU v7x, 16 devices: a 4x2x1 block of a 4x4x8 slice. The times are simulated.
16 devices in a mesh: replica: 2 (over y, z), vocab: 8 (over x, core).
Axes of the slice: x: 4, y: 2, z: 1, core: 2. Of those that a mesh axis runs over, the one named last changes fastest.
The devices are a block of a 4x4x8 slice.
Arguments:
- hidden: bfloat16 [1024, 1536], P(('replica', 'vocab')), parts along dimension 0
- w_head: bfloat16 [151936, 1536], P('vocab')
- allowed_ids: int32 [1024, 64], P(('replica', 'vocab')), parts along dimension 0
- allowed_valid: int32 [1024, 64], P(('replica', 'vocab')), parts along dimension 0
- target_pos: int32 [1024], P(('replica', 'vocab')), parts along dimension 0
Outputs:
- output 1: float32 [1024, 64], P(('replica', 'vocab')), parts along dimension 0
- output 2: float32 [1024], P(('replica', 'vocab')), parts along dimension 0
There are 2 independent parts. A program takes and returns all parts, laid end to end along the dimension named above; an argument that names none is the same for every part.
All inputs are finite; a program needn't handle non-finite values.
Results may differ from a plain program's by a relative error of at most 0.001.
Values are sent between devices in bfloat16 or wider.
A program may use at most 768 MiB of HBM per device.

v0:
```python
import jax
import jax.numpy as jnp
from jax import lax
from jax.sharding import PartitionSpec as P

value_a11 = 0.7


def finish_rows(scores, valid_in, tgt_in):
    valid_mask = valid_in > 0
    logits = jnp.where(valid_mask, scores, -jnp.inf)
    log_norm = jax.nn.logsumexp(logits, axis=1)
    allowed_prob = jnp.where(valid_mask, jnp.exp(logits - log_norm[:, None]), 0.0)
    tgt_hit = tgt_in[:, None] == jnp.arange(scores.shape[1])[None, :]
    target_logp = jnp.sum(jnp.where(tgt_hit, scores, 0.0), axis=1) - log_norm
    return allowed_prob, target_logp


def solution(mesh):
    groups = mesh.shape["vocab"]
    rows_spec = P(("replica", "vocab"), None)
    vec_spec = P(("replica", "vocab"))

    def local_step(h_loc, w_loc, ids_loc, valid_loc, tgt_loc):
        n_rows, list_len = ids_loc.shape
        shard_len = w_loc.shape[0]
        n_entries = n_rows * list_len
        capacity = n_rows * (list_len // 2)
        h_all = lax.all_gather(h_loc, "vocab", tiled=True)
        ids_flat = ids_loc.reshape(n_entries)
        keep_mask = valid_loc.reshape(n_entries) > 0
        owner_id = jnp.where(keep_mask, ids_flat // shard_len, groups)
        owner_hot = (owner_id[:, None] == jnp.arange(groups)[None, :]).astype(jnp.int32)
        slot_rank = jnp.sum(jnp.cumsum(owner_hot, axis=0) * owner_hot, axis=1) - 1
        dest_id = jnp.where(keep_mask, owner_id, 0)
        dest_slot = jnp.where(keep_mask, slot_rank, capacity)
        entry_row = jnp.arange(n_entries, dtype=jnp.int32) // list_len
        local_tok = ids_flat - owner_id * shard_len
        send_row = jnp.full((groups, capacity), -1, jnp.int32).at[dest_id, dest_slot].set(entry_row, mode="drop")
        send_tok = jnp.zeros((groups, capacity), jnp.int32).at[dest_id, dest_slot].set(local_tok, mode="drop")
        recv_buf = lax.all_to_all(jnp.stack([send_row, send_tok], axis=1), "vocab", 0, 0, tiled=True)
        recv_row = recv_buf[:, 0, :]
        filled = recv_row >= 0
        glob_row = jnp.arange(groups, dtype=jnp.int32)[:, None] * n_rows + jnp.maximum(recv_row, 0)
        w_rows = jnp.take(w_loc, recv_buf[:, 1, :], axis=0)
        h_rows = jnp.take(h_all, glob_row, axis=0)
        part_scores = jnp.einsum("pcd,pcd->pc", w_rows, h_rows, preferred_element_type=jnp.float32)
        part_scores = jnp.where(filled, part_scores, 0.0)
        back_buf = lax.all_to_all(part_scores, "vocab", 0, 0, tiled=True)
        flat_scores = back_buf[dest_id, jnp.clip(slot_rank, 0, capacity - 1)]
        scores = flat_scores.reshape(n_rows, list_len) / value_a11
        return finish_rows(scores, valid_loc, tgt_loc)

    mapped = jax.shard_map(local_step, mesh=mesh, in_specs=(rows_spec, P("vocab", None), rows_spec, rows_spec, vec_spec), out_specs=(rows_spec, vec_spec), check_vma=False)
    return mapped
```

profile of v0, /device:TPU:112, one launch (start us, length us, event | category | flops | bytes accessed | tf_op | source)
XLA Modules:
  0.0 1065.1 jit_solution(16064282717899004495)
XLA Ops:
  7.2 0.8 broadcast_compare_fusion
  8.1 0.8 fusion.8
  9.2 0.8 reshape.294
  10.0 0.8 broadcast_divide_fusion
  11.0 2.3 reduce-window.6
  13.3 0.3 slice_reduce_fusion
  14.1 0.7 fusion.15
  14.8 0.8 and_reduce_fusion
  15.6 0.8 multiply_reduce_fusion
  16.4 15.6 %scatter_custom_fusion.1 = s32[16384]{0:T(1024)S(1)} fusion(s32[4096]{0:T(1024)S(1)} %get-tuple-element.16, s32[4096]{0:T(1024)S(1)} %get-tuple-element.13, s32[]{:T(128)} %constant.40.clone.1), kind=kCustom, calls=%fused_computation.35 | custom fusion | bytes 65540
  31.9 15.6 %scatter_custom_fusion = s32[16384]{0:T(1024)S(1)} fusion(s32[4096]{0:T(1024)S(1)} %get-tuple-element.16, s32[4096]{0:T(1024)S(1)} %get-tuple-element.15, s32[]{:T(128)} %constant.41.clone.1), kind=kCustom, calls=%fused_computation.37 | custom fusion | bytes 65540
  47.5 0.7 pad_add_fusion
  48.2 5.3 all-to-all-start
  53.6 0.7 all-gather.2.cloned.1.call-update
  54.4 5.1 all-to-all-done
  59.4 0.2 compare_select_fusion.1
  59.7 601.1 %gather_fusion = bf16[16384,1536]{1,0:T(8,128)(2,1)} fusion(bf16[18992,1536]{1,0:T(8,128)(2,1)} %param.6, s32[16384]{0:T(1024)S(1)} %broadcast_clamp_fusion.1), kind=kCustom, calls=%fused_computation | custom fusion | bytes 100728832 | tf_op jit(solution)/shard_map/jit(_take)/gather | solution.py:45
  661.0 0.7 slice_compare_fusion
  661.7 99.0 %gather_fusion.1 = bf16[16384,1536]{1,0:T(8,128)(2,1)} fusion(bf16[512,1536]{1,0:T(8,128)(2,1)} %all-gather.2.cloned.1.call-done, s32[16384]{0:T(1024)S(1)} %broadcast_clamp_fusion), kind=kCustom, calls=%fused_computation.1 | custom fusion | bytes 100728832 | tf_op jit(solution)/shard_map/jit(_take)/gather | solution.py:46
  760.8 31.1 %fusion = f32[8,2048]{1,0:T(8,128)S(1)} fusion(bf16[8,2048,1536]{2,1,0:T(8,128)(2,1)} %bitcast.51, bf16[8,2048,1536]{2,1,0:T(8,128)(2,1)} %bitcast.50, pred[8,2048]{1,0:T(8,128)(4,1)S(1)} %compare_and_fusion, pred[8,2048]{1,0:T(8,128)(4,1)S(1)} %compare_and_fusion.1), kind=kLoop, calls=%fused_computation.6 | loop fusion | flops 150978560 | bytes 100761600 | tf_op jit(solution)/shard_map/pcd,pcd->pc/dot_general | solution.py:47
  792.0 239.1 %all_to_all.17 = f32[8,1,2048]{2,1,0:T(1,128)S(1)} all-to-all(f32[8,1,2048]{2,1,0:T(1,128)S(1)} %copy.7), channel_id=1, replica_groups=mesh['replica'=2,'vocab'=8] {'vocab'}, dimensions={0} | all-to-all | bytes 131072 | tf_op jit(solution)/shard_map/all_to_all | solution.py:49
  1031.1 25.5 %gather_fusion.2 = f32[4096]{0:T(1024)S(1)} fusion(f32[8,2048]{1,0:T(8,128)S(1)} %bitcast.48, s32[4096]{0:T(1024)S(1)} %bitcast.49), kind=kCustom, calls=%fused_computation.2 | custom fusion | bytes 65536 | tf_op jit(solution)/shard_map/gather | solution.py:50
  1057.0 0.5 fusion.19
  1057.5 0.7 exponential_select_fusion
  (39 shorter events, 1.9 us)
Async XLA Ops:
  48.2 11.2 %all-to-all-start = ((s32[8,2,2048]{2,1,0:T(2,128)}), s32[8,2,2048]{2,1,0:T(2,128)S(1)}, u32[]{:S(2)}, u32[]{:S(2)}) async-start(s32[8,2,2048]{2,1,0:T(2,128)} %pad_add_fusion), calls=%async_computation | async-start | bytes 262144 | tf_op jit(solution)/shard_map/all_to_all | solution.py:41
  53.5 608.2 %all-gather.2.cloned.1.call-start = ((), (), s32[]{:S(2)}) async-start(), calls=%async_computation.2 | async-start | bytes 1769472 | tf_op jit(solution)/shard_map/all_gather | solution.py:29
  760.7 31.1 %copy-start.2 = (pred[8,1,2048]{2,1,0:T(4,128)(4,1)S(1)}, pred[8,1,2048]{2,1,0:T(4,128)(4,1)}, u32[]{:S(2)}) copy-start(pred[8,1,2048]{2,1,0:T(4,128)(4,1)} %slice_compare_fusion) | copy-start | bytes 49156
  760.7 270.3 %copy-start = (s32[4096,1]{0,1:T(1,128)S(1)}, s32[4096,1]{0,1:T(1,128)}, u32[]{:S(2)}) copy-start(s32[4096,1]{0,1:T(1,128)} %get-tuple-element.6) | copy-start | bytes 49156
  760.7 295.9 %copy-start.1 = (s32[64,64]{1,0:T(8,128)S(1)}, s32[64,64]{1,0:T(8,128)}, u32[]{:S(2)}) copy-start(s32[64,64]{1,0:T(8,128)} %param.8) | copy-start | bytes 49156
  760.7 296.0 %copy-start.3 = (s32[64]{0:T(128)S(1)}, s32[64]{0:T(128)}, u32[]{:S(2)}) copy-start(s32[64]{0:T(128)} %param.9) | copy-start | bytes 772
Sparse Core Ops, SparseCore 0:
  56.0 22.5 all-gather.1
where the time goes:
time: 1080 us; the launch traced here: 1070 us
  local copies, waits for them, and re-layouts  759 us (70%)
  blocking collectives  239 us (22%)
  other arithmetic  42 us (4%)
  between operations  14.3 us (1%)
    gather x1, local copies, waits for them, and re-layouts, local_step(): w_rows = jnp.take(w_loc, recv_buf[:, 1, :], axis=0)  601 us
    all_to_all x1, blocking collectives, local_step(): back_buf = lax.all_to_all(part_scores, 'vocab', 0, 0, tiled=True)  239 us
    gather x1, local copies, waits for them, and re-layouts, local_step(): h_rows = jnp.take(h_all, glob_row, axis=0)  99 us
    unnamed x11, local copies, waits for them, and re-layouts  31.1 us
    dot_general x1, other arithmetic, local_step(): jnp.einsum('pcd,pcd->pc', w_rows, h_rows, preferred_element_type=jnp.floa...  31.1 us
    gather x1, local copies, waits for them, and re-layouts, local_step(): flat_scores = back_buf[dest_id, jnp.clip(slot_rank, 0, capacity - 1)]  25.5 us
  transfers between devices with their start and end apart: 2, of which 1 were waited for; matrix products, arithmetic and copies ran while one was open for 57% of the time, Pallas kernels for 0%

commit v1 on v0

v1 whole, which is shorter than its diff:
```python
import functools

import jax
import jax.numpy as jnp
from jax import lax
from jax.experimental import pallas as pl
from jax.experimental.pallas import tpu as pltpu
from jax.sharding import PartitionSpec as P

TEMP = 0.7
LANES = 128
TILE = 1024
BLOCK = 256


def score_tile(h_ref, w_ref, s_ref, rows):
    for start in range(0, rows, BLOCK):
        width = min(BLOCK, rows - start)
        s_ref[:, start : start + width] = lax.dot_general(
            h_ref[...], w_ref[start : start + width, :], (((1,), (1,)), ((), ())), preferred_element_type=jnp.float32
        )


def pick_tile(s_ref, lane_ref, chunk_ref, out_ref, first_chunk, rows):
    for g in range(0, out_ref.shape[0], 8):
        lane = lane_ref[g : g + 8, :]
        rel = chunk_ref[g : g + 8, :] - first_chunk
        acc = out_ref[g : g + 8, :]
        for c in range(-(-rows // LANES)):
            x = s_ref[g : g + 8, c * LANES : (c + 1) * LANES]
            got = jnp.take_along_axis(x, lane, axis=1, mode="promise_in_bounds")
            acc = jnp.where(rel == c, got, acc)
        out_ref[g : g + 8, :] = acc


def scores_kernel(h_ref, lane_ref, chunk_ref, w_hbm, out_ref, w0, w1, s0, s1, sem):
    shard = w_hbm.shape[0]
    pairs = shard // (2 * TILE)
    tail = shard - pairs * 2 * TILE
    out_ref[...] = jnp.zeros_like(out_ref)

    def copy(tile, buf, k):
        return pltpu.make_async_copy(w_hbm.at[pl.ds(tile * TILE, TILE), :], buf, sem.at[k])

    def tail_copy(buf):
        return pltpu.make_async_copy(w_hbm.at[pl.ds(pairs * 2 * TILE, tail), :], buf.at[pl.ds(0, tail), :], sem.at[0])

    copy(0, w0, 0).start()
    copy(1, w1, 1).start()
    s1[...] = jnp.zeros_like(s1)

    def body(i, _):
        copy(2 * i, w0, 0).wait()
        score_tile(h_ref, w0, s0, TILE)
        pick_tile(s1, lane_ref, chunk_ref, out_ref, (2 * i - 1) * (TILE // LANES), TILE)

        @pl.when(i + 1 < pairs)
        def _():
            copy(2 * i + 2, w0, 0).start()

        @pl.when(i + 1 == pairs)
        def _():
            tail_copy(w0).start()

        copy(2 * i + 1, w1, 1).wait()
        score_tile(h_ref, w1, s1, TILE)
        pick_tile(s0, lane_ref, chunk_ref, out_ref, 2 * i * (TILE // LANES), TILE)

        @pl.when(i + 1 < pairs)
        def _():
            copy(2 * i + 3, w1, 1).start()

        return 0

    lax.fori_loop(0, pairs, body, 0)
    tail_copy(w0).wait()
    score_tile(h_ref, w0, s0, tail)
    pick_tile(s1, lane_ref, chunk_ref, out_ref, (2 * pairs - 1) * (TILE // LANES), TILE)
    pick_tile(s0, lane_ref, chunk_ref, out_ref, 2 * pairs * (TILE // LANES), tail)


def all_scores(h_all, lane, chunk, w_loc):
    n_rows, width = h_all.shape
    vmem = pl.BlockSpec(memory_space=pltpu.VMEM)
    return pl.pallas_call(
        scores_kernel,
        out_shape=jax.ShapeDtypeStruct((n_rows, LANES), jnp.float32),
        in_specs=[vmem, vmem, vmem, pl.BlockSpec(memory_space=pl.ANY)],
        out_specs=vmem,
        scratch_shapes=[
            pltpu.VMEM((TILE, width), jnp.bfloat16),
            pltpu.VMEM((TILE, width), jnp.bfloat16),
            pltpu.VMEM((n_rows, TILE), jnp.float32),
            pltpu.VMEM((n_rows, TILE), jnp.float32),
            pltpu.SemaphoreType.DMA((2,)),
        ],
        compiler_params=pltpu.CompilerParams(vmem_limit_bytes=40 * 1024 * 1024),
        name="scores",
    )(h_all, lane, chunk, w_loc)


def finish_rows(scores, valid_in, tgt_in):
    valid_mask = valid_in > 0
    logits = jnp.where(valid_mask, scores, -jnp.inf)
    log_norm = jax.nn.logsumexp(logits, axis=1)
    allowed_prob = jnp.where(valid_mask, jnp.exp(logits - log_norm[:, None]), 0.0)
    tgt_hit = tgt_in[:, None] == jnp.arange(scores.shape[1])[None, :]
    target_logp = jnp.sum(jnp.where(tgt_hit, scores, 0.0), axis=1) - log_norm
    return allowed_prob, target_logp


def solution(mesh):
    groups = mesh.shape["vocab"]
    rows_spec = P(("replica", "vocab"), None)
    vec_spec = P(("replica", "vocab"))

    def local_step(h_loc, w_loc, ids_loc, valid_loc, tgt_loc):
        n_rows, list_len = ids_loc.shape
        shard_len = w_loc.shape[0]
        me = lax.axis_index("vocab")
        half = h_loc.shape[1] // 2
        h_all = jnp.concatenate(
            [lax.all_gather(h_loc[:, :half], "vocab", tiled=True), lax.all_gather(h_loc[:, half:], "vocab", tiled=True)], axis=1
        )
        ids_all = lax.all_gather(ids_loc, "vocab", tiled=True)
        local = ids_all - me * shard_len
        mine = (local >= 0) & (local < shard_len)
        chunk = jnp.where(mine, local // LANES, -(2**20))
        lane = jnp.where(mine, local % LANES, 0)
        pad = ((0, 0), (0, LANES - list_len))
        part = all_scores(h_all, jnp.pad(lane, pad), jnp.pad(chunk, pad, constant_values=-(2**20)), w_loc)
        part = part[:, :list_len].reshape(groups, n_rows, list_len)
        back = lax.all_to_all(part, "vocab", 0, 0, tiled=True)
        scores = jnp.sum(back, axis=0) / TEMP
        return finish_rows(scores, valid_loc, tgt_loc)

    return jax.shard_map(
        local_step,
        mesh=mesh,
        in_specs=(rows_spec, P("vocab", None), rows_spec, rows_spec, vec_spec),
        out_specs=(rows_spec, vec_spec),
        check_vma=False,
    )
```

time: 1080 us -> 122 us (0.11); the launches traced: 1070 us -> 121 us
  local copies, waits for them, and re-layouts: 759 us -> 1.8 us
  blocking collectives: 239 us -> 79.4 us
  other arithmetic: 42 us -> 2.88 us
  Pallas kernels: 0 us -> 36.4 us
  between operations: 14.3 us -> 0.75 us
    gather x3 -> x0, local copies, waits for them, and re-layouts: 726 us -> none  [the longest x1 601 us: local_step(): w_rows = jnp.take(w_loc, recv_buf[:, 1, :], axis=0)]
    all_to_all x1, blocking collectives: 239 us -> 8.65 us  [local_step(): back = lax.all_to_all(part, 'vocab', 0, 0, tiled=True)]
    all_gather x0 -> x3, blocking collectives: none -> 70.7 us  [the longest x1 25.4 us: local_step(): lax.all_gather(h_loc[:, half:], 'vocab', tiled=True)]
    pallas_call x0 -> x1, Pallas kernels: none -> 36.4 us  [all_scores(): pl.pallas_call(scores_kernel, out_shape=jax.ShapeDtypeStruct((n_rows, LAN...]
    dot_general x1 -> x0, other arithmetic: 31.1 us -> none  [local_step(): jnp.einsum('pcd,pcd->pc', w_rows, h_rows, preferred_element_type=jnp.floa...]
    unnamed x11 -> x6, local copies, waits for them, and re-layouts: 31.1 us -> 0.29 us
  transfers between devices with their start and end apart: 2 -> 0, of which waited for: 1 -> 0; matrix products, arithmetic and copies ran while one was open for 57% -> 0% of each run, Pallas kernels for 0% -> 0%
where the time goes in v1:
time: 122 us; the launch traced here: 121 us
  blocking collectives  79.4 us (65%)
  Pallas kernels  36.4 us (30%)
  other arithmetic  2.88 us (2%)
  local copies, waits for them, and re-layouts  1.8 us (1%)
    pallas_call x1, Pallas kernels, all_scores(): pl.pallas_call(scores_kernel, out_shape=jax.ShapeDtypeStruct((n_rows, LAN...  36.4 us
    all_gather x1, blocking collectives, local_step(): lax.all_gather(h_loc[:, half:], 'vocab', tiled=True)  25.4 us
    all_gather x1, blocking collectives, local_step(): ids_all = lax.all_gather(ids_loc, 'vocab', tiled=True)  23 us
    all_gather x1, blocking collectives, local_step(): lax.all_gather(h_loc[:, :half], 'vocab', tiled=True)  22.3 us
    all_to_all x1, blocking collectives, local_step(): back = lax.all_to_all(part, 'vocab', 0, 0, tiled=True)  8.65 us

profile of v1, /device:TPU:112, one launch (start us, length us, event | category | flops | bytes accessed | tf_op | source)
XLA Modules:
  0.0 121.2 jit_solution(15893434973869776267)
XLA Ops:
  0.6 1.0 fusion.6
  1.6 25.4 %all_gather.10 = bf16[512,768]{1,0:T(8,128)(2,1)S(1)} all-gather(bf16[64,768]{1,0:T(8,128)(2,1)S(1)} %get-tuple-element.11), channel_id=1, replica_groups=mesh['replica'=2,'vocab'=8] {'vocab'}, dimensions={0}, use_global_device_ids=true | all-gather | bytes 884736 | tf_op jit(solution)/shard_map/all_gather | solution.py:123
  27.0 22.3 %all_gather.9 = bf16[512,768]{1,0:T(8,128)(2,1)S(1)} all-gather(bf16[64,768]{1,0:T(8,128)(2,1)S(1)} %get-tuple-element.10), channel_id=1, replica_groups=mesh['replica'=2,'vocab'=8] {'vocab'}, dimensions={0}, use_global_device_ids=true | all-gather | bytes 884736 | tf_op jit(solution)/shard_map/all_gather | solution.py:123
  49.3 23.0 %all_gather.11 = s32[512,64]{1,0:T(8,128)S(1)} all-gather(s32[64,64]{1,0:T(8,128)} %param.7), channel_id=1, replica_groups=mesh['replica'=2,'vocab'=8] {'vocab'}, dimensions={0}, use_global_device_ids=true | all-gather | bytes 147456 | tf_op jit(solution)/shard_map/all_gather | solution.py:125
  72.3 0.1 pad_maximum_fusion.h_ref
  72.4 0.3 fusion.1
  72.8 0.0 copy-start
  72.8 0.0 copy-start.1
  72.8 36.4 %scores.1 = f32[512,128]{1,0:T(8,128)S(1)} custom-call(bf16[512,1536]{1,0:T(8,128)(2,1)S(1)} %pad_maximum_fusion.h_ref, s32[512,128]{1,0:T(8,128)S(1)} %pad.7.lane_ref, s32[512,128]{1,0:T(8,128)S(1)} %pad.8.chunk_ref, bf16[18992,1536]{1,0:T(8,128)(2,1)} %w_hbm.1), custom_call_target="tpu_custom_call" | custom-call | tf_op jit(solution)/shard_map/scores/pallas_call | solution.py:85
  109.2 0.2 reshape.20
  109.4 8.7 %all_to_all.5 = f32[8,1,4096]{2,1,0:T(1,128)S(1)} all-to-all(f32[8,1,4096]{2,1,0:T(1,128)S(1)} %reshape.20), channel_id=1, replica_groups=mesh['replica'=2,'vocab'=8] {'vocab'}, dimensions={0} | all-to-all | bytes 262144 | tf_op jit(solution)/shard_map/all_to_all | solution.py:133
  118.1 0.5 broadcast.22
  118.6 1.0 reduce
  119.5 0.1 reshape.21
  119.7 0.0 copy-done
  119.7 0.1 fusion.4
  119.8 0.0 copy-done.1
  119.8 0.2 select_reduce_fusion
  120.0 0.5 fusion.5
  120.5 0.7 exponential_select_fusion
  (4 shorter events, 0.1 us)
Async XLA Ops:
  72.8 46.9 %copy-start = (s32[64,64]{1,0:T(8,128)S(1)}, s32[64,64]{1,0:T(8,128)}, u32[]{:S(2)}) copy-start(s32[64,64]{1,0:T(8,128)} %param.8) | copy-start | bytes 49156
  72.8 47.0 %copy-start.1 = (s32[64]{0:T(128)S(1)}, s32[64]{0:T(128)}, u32[]{:S(2)}) copy-start(s32[64]{0:T(128)} %param.9) | copy-start | bytes 772

commit v2 on v1

v2 whole, which is shorter than its diff:
```python
import functools

import jax
import jax.numpy as jnp
from jax import lax
from jax.experimental import pallas as pl
from jax.experimental.pallas import tpu as pltpu
from jax.sharding import PartitionSpec as P

TEMP = 0.7
LANES = 128
TILE = 1024
BLOCK = 256
FAR = -(2**20)
PIECES = 16

SELF, PARTNER = 0, 2
LEFT_A, RIGHT_B = 4, 6
LEFT_B, RIGHT_A = 8, 10
ACROSS_A, ACROSS_B = 12, 14


def score_tile(h_ref, w_ref, s_ref, rows):
    for start in range(0, rows, BLOCK):
        width = min(BLOCK, rows - start)
        s_ref[:, start : start + width] = lax.dot_general(
            h_ref[...], w_ref[start : start + width, :], (((1,), (1,)), ((), ())), preferred_element_type=jnp.float32
        )


def pick_tile(s_ref, lane_ref, chunk_ref, out_ref, first_chunk, rows):
    low = lax.broadcasted_iota(jnp.int32, (8, LANES), 1) < LANES // 2
    for u in range(out_ref.shape[0] // 8):
        at = pl.ds(8 * u, 8)
        lane = lane_ref[at, :]
        rel = chunk_ref[at, :] - first_chunk
        acc = out_ref[at, :]
        for c in range(-(-rows // LANES)):
            cols = pl.ds(c * LANES, LANES)
            first = jnp.take_along_axis(s_ref[pl.ds(16 * u, 8), cols], lane, axis=1, mode="promise_in_bounds")
            second = jnp.take_along_axis(s_ref[pl.ds(16 * u + 8, 8), cols], lane, axis=1, mode="promise_in_bounds")
            acc = jnp.where(rel == c, jnp.where(low, first, second), acc)
        out_ref[at, :] = acc


def kernel(
    chips, h_ref, ids_ref, valid_ref, tgt_ref, w_hbm, p_ref, lp_ref,
    h_all, ids_all, chunk, lane, acc, back, w0, w1, s0, s1,
    w_sem, h_send, h_recv, i_send, i_recv, x_send, x_recv,
):
    n_rows, list_len = ids_ref.shape
    half = n_rows // 2
    packed = half // 2
    shard = w_hbm.shape[0]
    pairs = shard // (2 * TILE)
    tail = shard - pairs * 2 * TILE
    me = lax.axis_index("vocab")
    chip, core = me // 2, me % 2

    def place(hop, other):
        return {"vocab": lax.rem(chip + hop, chips) * 2 + (1 - core if other else core)}

    right, left, partner = place(1, False), place(chips - 1, False), place(0, True)

    def w_copy(tile, buf, k):
        return pltpu.make_async_copy(w_hbm.at[pl.ds(tile * TILE, TILE), :], buf, w_sem.at[k])

    def tail_copy(buf):
        return pltpu.make_async_copy(w_hbm.at[pl.ds(pairs * 2 * TILE, tail), :], buf.at[pl.ds(0, tail), :], w_sem.at[0])

    w_copy(0, w0, 0).start()
    w_copy(1, w1, 1).start()
    own = pltpu.make_async_copy(h_ref, h_all.at[pl.ds(0, n_rows), :], w_sem.at[2])
    own.start()
    barrier = pltpu.get_barrier_semaphore()
    for peer in (left, right, partner):
        pl.semaphore_signal(barrier, inc=1, device_id=peer, device_id_type=pl.DeviceIdType.MESH)

    listed = jnp.where(valid_ref[...] > 0, ids_ref[...], -1)
    for k in range(n_rows // 16):
        ids_all[pl.ds(8 * k, 8), :] = jnp.concatenate([listed[16 * k : 16 * k + 8], listed[16 * k + 8 : 16 * k + 16]], axis=1)
    acc[...] = jnp.zeros_like(acc)
    s1[...] = jnp.zeros_like(s1)
    pl.semaphore_wait(barrier, 3)

    sent = []

    def send(src, dst, count, peer):
        rows_h = h_ref.at[pl.ds(src * half, count * half), :] if src < PARTNER else h_all.at[pl.ds(src * half, half), :]
        copy_h = pltpu.make_async_remote_copy(
            src_ref=rows_h, dst_ref=h_all.at[pl.ds(dst * half, count * half), :],
            send_sem=h_send.at[len(sent)], recv_sem=h_recv.at[dst], device_id=peer, device_id_type=pl.DeviceIdType.MESH,
        )
        copy_i = pltpu.make_async_remote_copy(
            src_ref=ids_all.at[pl.ds(src * packed, count * packed), :], dst_ref=ids_all.at[pl.ds(dst * packed, count * packed), :],
            send_sem=i_send.at[len(sent)], recv_sem=i_recv.at[dst], device_id=peer, device_id_type=pl.DeviceIdType.MESH,
        )
        copy_h.start()
        copy_i.start()
        sent.append((copy_h, copy_i))

    def arrived(dst, count=1):
        pltpu.make_async_copy(h_all.at[pl.ds(dst * half, count * half), :], h_all.at[pl.ds(dst * half, count * half), :], h_recv.at[dst]).wait()
        pltpu.make_async_copy(ids_all.at[pl.ds(dst * packed, count * packed), :], ids_all.at[pl.ds(dst * packed, count * packed), :], i_recv.at[dst]).wait()

    send(0, LEFT_A, 1, right)
    send(1, RIGHT_B, 1, left)
    send(0, PARTNER, 2, partner)
    send(1, LEFT_B, 1, right)
    send(0, RIGHT_A, 1, left)
    arrived(LEFT_A)
    send(LEFT_A, ACROSS_A, 1, right)
    send(LEFT_A, LEFT_A + 1, 1, partner)
    arrived(RIGHT_B)
    send(RIGHT_B, ACROSS_B, 1, left)
    send(RIGHT_B, RIGHT_B + 1, 1, partner)
    for piece in (LEFT_B, RIGHT_A, ACROSS_A, ACROSS_B):
        arrived(piece)
        send(piece, piece + 1, 1, partner)
    arrived(PARTNER, 2)
    for piece in (LEFT_A, RIGHT_B, LEFT_B, RIGHT_A, ACROSS_A, ACROSS_B):
        arrived(piece + 1)
    own.wait()

    for u in range(PIECES * packed // 8):
        at = pl.ds(8 * u, 8)
        local = ids_all[at, :] - me * shard
        mine = (local >= 0) & (local < shard)
        chunk[at, :] = jnp.where(mine, lax.shift_right_arithmetic(local, 7), FAR)
        lane[at, :] = local & (LANES - 1)

    def body(i, _):
        w_copy(2 * i, w0, 0).wait()
        score_tile(h_all, w0, s0, TILE)
        pick_tile(s1, lane, chunk, acc, (2 * i - 1) * (TILE // LANES), TILE)

        @pl.when(i + 1 < pairs)
        def _():
            w_copy(2 * i + 2, w0, 0).start()

        @pl.when(i + 1 == pairs)
        def _():
            tail_copy(w0).start()

        w_copy(2 * i + 1, w1, 1).wait()
        score_tile(h_all, w1, s1, TILE)
        pick_tile(s0, lane, chunk, acc, 2 * i * (TILE // LANES), TILE)

        @pl.when(i + 1 < pairs)
        def _():
            w_copy(2 * i + 3, w1, 1).start()

        return 0

    lax.fori_loop(0, pairs, body, 0)
    tail_copy(w0).wait()
    score_tile(h_all, w0, s0, tail)
    pick_tile(s1, lane, chunk, acc, (2 * pairs - 1) * (TILE // LANES), TILE)
    pick_tile(s0, lane, chunk, acc, 2 * pairs * (TILE // LANES), tail)

    exits = []
    for hop, first, second in ((2, ACROSS_A, ACROSS_B), (chips - 1, LEFT_A, LEFT_B), (1, RIGHT_A, RIGHT_B), (0, PARTNER, PARTNER + 1)):
        for other in (False, True):
            if hop == 0 and not other:
                continue
            slot = ((chips - hop) % chips) * 2 + int(other)
            for part, piece in enumerate((first, second)):
                shift = int(other) if hop else 0
                out = pltpu.make_async_remote_copy(
                    src_ref=acc.at[pl.ds((piece + shift) * packed, packed), :],
                    dst_ref=back.at[slot, pl.ds(part * packed, packed), :],
                    send_sem=x_send.at[2 * slot + part], recv_sem=x_recv.at[2 * slot + part],
                    device_id=place(hop, other), device_id_type=pl.DeviceIdType.MESH,
                )
                out.start()
                exits.append(out)
    total = acc[pl.ds(0, 2 * packed), :]
    for out in exits:
        out.wait()
    for slot in range(1, 2 * chips):
        total = total + back[slot]

    rows = []
    for k in range(n_rows // 16):
        rows += [total[8 * k : 8 * k + 8, :list_len], total[8 * k : 8 * k + 8, list_len:]]
    scores = jnp.concatenate(rows, axis=0) / TEMP
    keep = valid_ref[...] > 0
    logits = jnp.where(keep, scores, -jnp.inf)
    top = jnp.max(logits, axis=1, keepdims=True)
    log_norm = top + jnp.log(jnp.sum(jnp.exp(logits - top), axis=1, keepdims=True))
    p_ref[...] = jnp.where(keep, jnp.exp(logits - log_norm), 0.0)
    row_id = lax.broadcasted_iota(jnp.int32, (n_rows, n_rows), 0)
    col_id = lax.broadcasted_iota(jnp.int32, (n_rows, n_rows), 1)
    eye = row_id == col_id
    target = jnp.sum(jnp.where(eye, jnp.broadcast_to(tgt_ref[...].astype(jnp.float32), (n_rows, n_rows)), 0.0), axis=1, keepdims=True)
    place_id = lax.broadcasted_iota(jnp.int32, (n_rows, list_len), 1).astype(jnp.float32)
    picked = jnp.sum(jnp.where(place_id == target, scores, 0.0), axis=1, keepdims=True)
    lp = picked - log_norm
    lp_ref[...] = jnp.sum(jnp.where(eye, jnp.broadcast_to(lp, (n_rows, n_rows)), 0.0), axis=0, keepdims=True)
    for copy_h, copy_i in sent:
        copy_h.wait_send()
        copy_i.wait_send()


def solution(mesh):
    groups = mesh.shape["vocab"]
    rows_spec = P(("replica", "vocab"), None)
    vec_spec = P(("replica", "vocab"))

    def local_step(h_loc, w_loc, ids_loc, valid_loc, tgt_loc):
        n_rows, list_len = ids_loc.shape
        width = h_loc.shape[1]
        all_rows = groups * n_rows
        vmem = pl.BlockSpec(memory_space=pltpu.VMEM)
        n_sent = 13
        p, lp = pl.pallas_call(
            functools.partial(kernel, groups // 2),
            out_shape=(jax.ShapeDtypeStruct((n_rows, list_len), jnp.float32), jax.ShapeDtypeStruct((1, n_rows), jnp.float32)),
            in_specs=[vmem, vmem, vmem, vmem, pl.BlockSpec(memory_space=pl.ANY)],
            out_specs=(vmem, vmem),
            scratch_shapes=[
                pltpu.VMEM((all_rows, width), jnp.bfloat16),
                pltpu.VMEM((all_rows // 2, LANES), jnp.int32),
                pltpu.VMEM((all_rows // 2, LANES), jnp.int32),
                pltpu.VMEM((all_rows // 2, LANES), jnp.int32),
                pltpu.VMEM((all_rows // 2, LANES), jnp.float32),
                pltpu.VMEM((groups, n_rows // 2, LANES), jnp.float32),
                pltpu.VMEM((TILE, width), jnp.bfloat16),
                pltpu.VMEM((TILE, width), jnp.bfloat16),
                pltpu.VMEM((all_rows, TILE), jnp.float32),
                pltpu.VMEM((all_rows, TILE), jnp.float32),
                pltpu.SemaphoreType.DMA((3,)),
                pltpu.SemaphoreType.DMA((n_sent,)),
                pltpu.SemaphoreType.DMA((PIECES,)),
                pltpu.SemaphoreType.DMA((n_sent,)),
                pltpu.SemaphoreType.DMA((PIECES,)),
                pltpu.SemaphoreType.DMA((2 * groups,)),
                pltpu.SemaphoreType.DMA((2 * groups,)),
            ],
            compiler_params=pltpu.CompilerParams(vmem_limit_bytes=48 * 1024 * 1024, collective_id=0, has_side_effects=True),
            name="fused",
        )(h_loc, ids_loc, valid_loc, tgt_loc.reshape(1, n_rows), w_loc)
        return p, lp.reshape(n_rows)

    return jax.shard_map(
        local_step,
        mesh=mesh,
        in_specs=(rows_spec, P("vocab", None), rows_spec, rows_spec, vec_spec),
        out_specs=(rows_spec, vec_spec),
        check_vma=False,
    )
```

time: 122 us -> 58.7 us (0.48)
  blocking collectives: 79.4 us -> 0 us
  Pallas kernels: 36.4 us -> 53.6 us
  other arithmetic: 2.88 us -> 0 us
  local copies, waits for them, and re-layouts: 1.8 us -> 4.22 us
    all_gather x3 -> x0, blocking collectives: 70.7 us -> none  [the longest x1 25.4 us: local_step(): lax.all_gather(h_loc[:, half:], 'vocab', tiled=True)]
    pallas_call x1, Pallas kernels: 36.4 us -> 53.6 us  [local_step(): pl.pallas_call(functools.partial(kernel, groups // 2), out_shape=(jax.Sha...]
    all_to_all x1 -> x0, blocking collectives: 8.65 us -> none  [local_step(): back = lax.all_to_all(part, 'vocab', 0, 0, tiled=True)]
    unnamed x6 -> x10, local copies, waits for them, and re-layouts: 0.29 us -> 4.22 us
where the time goes in v2:
time: 58.7 us; the launch traced here: 58.5 us
  Pallas kernels  53.6 us (91%)
  local copies, waits for them, and re-layouts  4.22 us (7%)
  between operations  0.65 us (1%)
    pallas_call x1, Pallas kernels, local_step(): pl.pallas_call(functools.partial(kernel, groups // 2), out_shape=(jax.Sha...  53.6 us
    unnamed x10, local copies, waits for them, and re-layouts  4.22 us

profile of v2, /device:TPU:112, one launch (start us, length us, event | category | flops | bytes accessed | tf_op | source)
XLA Modules:
  0.0 58.5 jit_solution(13791068815988481137)
XLA Ops:
  0.6 0.0 copy-start
  0.6 0.9 %copy-done = bf16[64,1536]{1,0:T(8,128)(2,1)S(1)} copy-done((bf16[64,1536]{1,0:T(8,128)(2,1)S(1)}, bf16[64,1536]{1,0:T(8,128)(2,1)}, u32[]{:S(2)}) %copy-start) | copy-done | bytes 196632
  1.6 0.0 copy-start.1
  1.6 0.8 %copy-done.1 = s32[64,64]{1,0:T(8,128)S(1)} copy-done((s32[64,64]{1,0:T(8,128)S(1)}, s32[64,64]{1,0:T(8,128)}, u32[]{:S(2)}) %copy-start.1) | copy-done | bytes 16408
  2.3 0.0 copy-start.2
  2.3 0.8 %copy-done.2 = s32[64,64]{1,0:T(8,128)S(1)} copy-done((s32[64,64]{1,0:T(8,128)S(1)}, s32[64,64]{1,0:T(8,128)}, u32[]{:S(2)}) %copy-start.2) | copy-done | bytes 16408
  3.1 0.0 copy-start.3
  3.1 0.7 %copy-done.3 = s32[64]{0:T(128)S(1)} copy-done((s32[64]{0:T(128)S(1)}, s32[64]{0:T(128)}, u32[]{:S(2)}) %copy-start.3) | copy-done | bytes 280
  3.7 53.6 %fused.1 = (f32[64,64]{1,0:T(8,128)S(1)}, f32[1,64]{1,0:T(1,128)S(1)}) custom-call(bf16[64,1536]{1,0:T(8,128)(2,1)S(1)} %copy-done, s32[64,64]{1,0:T(8,128)S(1)} %copy-done.1, s32[64,64]{1,0:T(8,128)S(1)} %copy-done.2, s32[1,64]{1,0:T(1,128)S(1)} %bitcast.2, bf16[18992,1536]{1,0:T(8,128)(2,1)} %w_hbm.1), custom_call_target="tpu_custom_call" | custom-call | tf_op jit(solution)/shard_map/fused/pallas_call | solution.py:216
  57.4 0.6 %copy.9 = f32[64,64]{1,0:T(8,128)} copy(f32[64,64]{1,0:T(8,128)S(1)} %get-tuple-element.8) | data formatting | bytes 32768
  58.0 0.5 copy.10
Async XLA Ops:
  0.6 0.9 %copy-start = (bf16[64,1536]{1,0:T(8,128)(2,1)S(1)}, bf16[64,1536]{1,0:T(8,128)(2,1)}, u32[]{:S(2)}) copy-start(bf16[64,1536]{1,0:T(8,128)(2,1)} %h_ref.1) | copy-start | bytes 589828
  1.6 0.8 %copy-start.1 = (s32[64,64]{1,0:T(8,128)S(1)}, s32[64,64]{1,0:T(8,128)}, u32[]{:S(2)}) copy-start(s32[64,64]{1,0:T(8,128)} %ids_ref.1) | copy-start | bytes 49156
  2.3 0.8 %copy-start.2 = (s32[64,64]{1,0:T(8,128)S(1)}, s32[64,64]{1,0:T(8,128)}, u32[]{:S(2)}) copy-start(s32[64,64]{1,0:T(8,128)} %valid_ref.1) | copy-start | bytes 49156
  3.1 0.7 %copy-start.3 = (s32[64]{0:T(128)S(1)}, s32[64]{0:T(128)}, u32[]{:S(2)}) copy-start(s32[64]{0:T(128)} %param.9) | copy-start | bytes 772

commit v3 on v2

v3 whole, which is shorter than its diff:
```python
import functools

import jax
import jax.numpy as jnp
from jax import lax
from jax.experimental import pallas as pl
from jax.experimental.pallas import tpu as pltpu
from jax.sharding import PartitionSpec as P

TEMP = 0.7
LANES = 128
TILE = 1024
BLOCK = 256
CHUNKS = TILE // LANES
FAR = -(2**20)
NEVER = 2**21
PIECES = 16
SLOTS = 12
EARLY_CHIP = 4
EARLY_HALF = 6
AHEAD = 3
MESH = pl.DeviceIdType.MESH

PARTNER = 2
LEFT_A, RIGHT_B = 4, 6
LEFT_B, RIGHT_A = 8, 10
ACROSS_A, ACROSS_B = 12, 14


def score_tile(h_ref, w_ref, slot, s_ref, lo, hi, rows):
    for start in range(0, rows, BLOCK):
        width = min(BLOCK, rows - start)
        s_ref[lo:hi, start : start + width] = lax.dot_general(
            h_ref[lo:hi, :], w_ref[slot, start : start + width, :], (((1,), (1,)), ((), ())), preferred_element_type=jnp.float32
        )


def permute(x, lane):
    dims = lax.GatherDimensionNumbers(
        offset_dims=(), collapsed_slice_dims=(1,), start_index_map=(1,), operand_batching_dims=(0,), start_indices_batching_dims=(0,)
    )
    return lax.gather(x, lane[:, :, None], dims, (1, 1), mode=lax.GatherScatterMode.PROMISE_IN_BOUNDS)


def pick_tile(s_ref, lane_ref, chunk_ref, out_ref, lo, hi, first_chunk, rows):
    low = lax.broadcasted_iota(jnp.int32, (8, LANES), 1) < LANES // 2
    for u in range(lo // 16, hi // 16):
        at = pl.ds(8 * u, 8)
        row = 32 * (u // 2) + 8 * (u % 2)
        lane = lane_ref[at, :]
        rel = chunk_ref[at, :] - first_chunk
        acc = out_ref[at, :]
        for c in range(-(-rows // LANES)):
            cols = pl.ds(c * LANES, LANES)
            first = permute(s_ref[pl.ds(row, 8), cols], lane)
            second = permute(s_ref[pl.ds(row + 16, 8), cols], lane)
            acc = jnp.where(rel == c, jnp.where(low, first, second), acc)
        out_ref[at, :] = acc


def kernel(
    chips, h_hbm, ids_hbm, valid_hbm, tgt_hbm, w_hbm, p_ref, lp_ref,
    h_all, ids_in, valid_in, tgt_in, ids_all, chunk, lane, acc, back, wbuf, s0, s1,
    in_sem, w_sem, h_send, h_recv, i_send, i_recv, x_send, x_recv,
):
    n_rows, list_len = ids_in.shape
    half = n_rows // 2
    packed = half // 2
    all_rows = h_all.shape[0]
    shard = w_hbm.shape[0]
    full = shard // TILE
    tail = shard - full * TILE
    me = lax.axis_index("vocab")
    chip, core = me // 2, me % 2

    def place(hop, other):
        return {"vocab": lax.rem(chip + hop, chips) * 2 + (1 - core if other else core)}

    right, left, partner = place(1, False), place(chips - 1, False), place(0, True)

    def w_copy(tile):
        slot = lax.rem(tile, SLOTS)
        return pltpu.make_async_copy(w_hbm.at[pl.ds(tile * TILE, TILE), :], wbuf.at[slot], w_sem.at[slot])

    def tail_copy():
        slot = full % SLOTS
        return pltpu.make_async_copy(w_hbm.at[pl.ds(full * TILE, tail), :], wbuf.at[slot, pl.ds(0, tail), :], w_sem.at[slot])

    inputs = [
        pltpu.make_async_copy(h_hbm, h_all.at[pl.ds(0, n_rows), :], in_sem.at[0]),
        pltpu.make_async_copy(ids_hbm, ids_in, in_sem.at[1]),
        pltpu.make_async_copy(valid_hbm, valid_in, in_sem.at[2]),
        pltpu.make_async_copy(tgt_hbm, tgt_in, in_sem.at[3]),
    ]
    for copy in inputs:
        copy.start()
    for t in range(AHEAD):
        w_copy(t).start()
    barrier = pltpu.get_barrier_semaphore()
    for peer in (left, right, partner):
        pl.semaphore_signal(barrier, inc=1, device_id=peer, device_id_type=MESH)
    acc[...] = jnp.zeros_like(acc)
    s1[...] = jnp.zeros_like(s1)
    inputs[1].wait()
    inputs[2].wait()
    listed = jnp.where(valid_in[...] > 0, ids_in[...], -1)
    for k in range(2):
        ids_all[pl.ds(packed * k, packed), :] = jnp.concatenate(
            [listed[half * k : half * k + packed], listed[half * k + packed : half * (k + 1)]], axis=1
        )
    pl.semaphore_wait(barrier, 3)
    inputs[0].wait()

    def hop(k, src, dst, count, peer):
        return (
            pltpu.make_async_remote_copy(
                src_ref=h_all.at[pl.ds(src * half, count * half), :], dst_ref=h_all.at[pl.ds(dst * half, count * half), :],
                send_sem=h_send.at[k], recv_sem=h_recv.at[dst], device_id=peer, device_id_type=MESH,
            ),
            pltpu.make_async_remote_copy(
                src_ref=ids_all.at[pl.ds(src * packed, count * packed), :], dst_ref=ids_all.at[pl.ds(dst * packed, count * packed), :],
                send_sem=i_send.at[k], recv_sem=i_recv.at[dst], device_id=peer, device_id_type=MESH,
            ),
        )

    sent = []

    def send(*moves):
        started = []
        for move in moves:
            args = (len(sent), *move)
            sent.append(args)
            started.append(hop(*args))
        for which in range(2):
            for pair in started:
                pair[which].start()

    def arrived(dst, count=1):
        for ref, size, sem in ((h_all, half, h_recv), (ids_all, packed, i_recv)):
            there = ref.at[pl.ds(dst * size, count * size), :]
            pltpu.make_async_copy(there, there, sem.at[dst]).wait()

    def prepare(first, last):
        at = pl.ds(first * packed, (last - first) * packed)
        local = ids_all[at, :] - me * shard
        mine = (local >= 0) & (local < shard)
        chunk[at, :] = jnp.where(mine, lax.shift_right_arithmetic(local, 7), FAR)
        lane[at, :] = local & (LANES - 1)

    def neighbours_first():
        arrived(LEFT_A)
        send((LEFT_A, ACROSS_A, 1, right), (LEFT_A, LEFT_A + 1, 1, partner))
        arrived(RIGHT_B)
        send((RIGHT_B, ACROSS_B, 1, left), (RIGHT_B, RIGHT_B + 1, 1, partner))

    def pass_on(*pieces):
        for piece in pieces:
            arrived(piece)
            send((piece, piece + 1, 1, partner))

    def phase(first, count, lo, hi, wait=True, ahead=False, refill=False, events={}):
        def body(i, _):
            t = first + 2 * i
            for when, event in events.items():
                pl.when(i == when)(event)
            if wait:
                w_copy(t).wait()
            if ahead:
                for k in range(2):
                    pl.when(t + AHEAD + k < SLOTS)(w_copy(t + AHEAD + k).start)
            score_tile(h_all, wbuf, lax.rem(t, SLOTS), s0, lo, hi, TILE)
            pick_tile(s1, lane, chunk, acc, lo, hi, jnp.where(i > 0, (t - 1) * CHUNKS, NEVER), TILE)
            if wait:
                w_copy(t + 1).wait()
            score_tile(h_all, wbuf, lax.rem(t + 1, SLOTS), s1, lo, hi, TILE)
            pick_tile(s0, lane, chunk, acc, lo, hi, t * CHUNKS, TILE)
            if refill:
                for k in range(2):
                    pl.when(t + k + SLOTS < full)(w_copy(t + k + SLOTS).start)
                    pl.when(t + k + SLOTS == full)(tail_copy().start)
            return 0

        lax.fori_loop(0, count // 2, body, 0)

    def last_pick(tile, lo, hi):
        pick_tile(s1, lane, chunk, acc, lo, hi, tile * CHUNKS, TILE)

    early = EARLY_CHIP + EARLY_HALF
    send((0, LEFT_A, 1, right), (1, RIGHT_B, 1, left), (0, PARTNER, 2, partner), (1, LEFT_B, 1, right), (0, RIGHT_A, 1, left))
    prepare(0, 2)
    arrived(PARTNER, 2)
    prepare(PARTNER, PARTNER + 2)
    phase(0, EARLY_CHIP, 0, all_rows // 4, ahead=True, events={1: neighbours_first})
    last_pick(EARLY_CHIP - 1, 0, all_rows // 4)
    arrived(LEFT_A + 1)
    arrived(RIGHT_B + 1)
    prepare(LEFT_A, RIGHT_B + 2)
    phase(
        EARLY_CHIP, EARLY_HALF, 0, all_rows // 2, ahead=True,
        events={1: lambda: pass_on(LEFT_B, RIGHT_A), 2: lambda: pass_on(ACROSS_A, ACROSS_B)},
    )
    last_pick(early - 1, 0, all_rows // 2)
    for piece in (LEFT_B, RIGHT_A, ACROSS_A, ACROSS_B):
        arrived(piece + 1)
    prepare(LEFT_B, PIECES)
    phase(0, EARLY_CHIP, all_rows // 4, all_rows, wait=False, refill=True)
    last_pick(EARLY_CHIP - 1, all_rows // 4, all_rows)
    phase(EARLY_CHIP, EARLY_HALF, all_rows // 2, all_rows, wait=False, refill=True)
    last_pick(early - 1, all_rows // 2, all_rows)
    phase(early, full - early, 0, all_rows)
    tail_copy().wait()
    score_tile(h_all, wbuf, full % SLOTS, s0, 0, all_rows, tail)
    last_pick(full - 1, 0, all_rows)
    pick_tile(s0, lane, chunk, acc, 0, all_rows, full * CHUNKS, tail)

    exits = []
    for hops, first, second in ((2, ACROSS_A, ACROSS_B), (chips - 1, LEFT_A, LEFT_B), (1, RIGHT_A, RIGHT_B), (0, PARTNER, PARTNER + 1)):
        for other in (False, True):
            if hops == 0 and not other:
                continue
            slot = ((chips - hops) % chips) * 2 + int(other)
            for part, piece in enumerate((first, second)):
                shift = int(other) if hops else 0
                out = pltpu.make_async_remote_copy(
                    src_ref=acc.at[pl.ds((piece + shift) * packed, packed), :],
                    dst_ref=back.at[slot, pl.ds(part * packed, packed), :],
                    send_sem=x_send.at[2 * slot + part], recv_sem=x_recv.at[2 * slot + part],
                    device_id=place(hops, other), device_id_type=MESH,
                )
                out.start()
                exits.append(out)
    inputs[3].wait()
    keep = valid_in[...] > 0
    row_id = lax.broadcasted_iota(jnp.int32, (n_rows, n_rows), 0)
    col_id = lax.broadcasted_iota(jnp.int32, (n_rows, n_rows), 1)
    eye = row_id == col_id
    target = jnp.sum(jnp.where(eye, jnp.broadcast_to(tgt_in[...].astype(jnp.float32), (n_rows, n_rows)), 0.0), axis=1, keepdims=True)
    total = acc[pl.ds(0, 2 * packed), :]
    for args in sent:
        for copy in hop(*args):
            copy.wait_send()
    for out in exits:
        out.wait()
    for slot in range(1, 2 * chips):
        total = total + back[slot]

    rows = []
    for k in range(2):
        rows += [total[packed * k : packed * (k + 1), :list_len], total[packed * k : packed * (k + 1), list_len:]]
    scores = jnp.concatenate(rows, axis=0) / TEMP
    logits = jnp.where(keep, scores, -jnp.inf)
    top = jnp.max(logits, axis=1, keepdims=True)
    log_norm = top + jnp.log(jnp.sum(jnp.exp(logits - top), axis=1, keepdims=True))
    p_ref[...] = jnp.where(keep, jnp.exp(logits - log_norm), 0.0)
    place_id = lax.broadcasted_iota(jnp.int32, (n_rows, list_len), 1).astype(jnp.float32)
    picked = jnp.sum(jnp.where(place_id == target, scores, 0.0), axis=1, keepdims=True)
    lp = picked - log_norm
    lp_ref[...] = jnp.sum(jnp.where(eye, jnp.broadcast_to(lp, (n_rows, n_rows)), 0.0), axis=0, keepdims=True)


def solution(mesh):
    groups = mesh.shape["vocab"]
    rows_spec = P(("replica", "vocab"), None)
    vec_spec = P(("replica", "vocab"))

    def local_step(h_loc, w_loc, ids_loc, valid_loc, tgt_loc):
        n_rows, list_len = ids_loc.shape
        width = h_loc.shape[1]
        all_rows = groups * n_rows
        vmem = pl.BlockSpec(memory_space=pltpu.VMEM)
        hbm = pl.BlockSpec(memory_space=pltpu.HBM)
        lists = pltpu.VMEM((all_rows // 2, LANES), jnp.int32)
        scores = pltpu.VMEM((all_rows, TILE), jnp.float32)
        sems = pltpu.SemaphoreType.DMA
        p, lp = pl.pallas_call(
            functools.partial(kernel, groups // 2),
            out_shape=(jax.ShapeDtypeStruct((n_rows, list_len), jnp.float32), jax.ShapeDtypeStruct((1, n_rows), jnp.float32)),
            in_specs=[hbm] * 5,
            out_specs=(vmem, vmem),
            scratch_shapes=[
                pltpu.VMEM((all_rows, width), jnp.bfloat16),
                pltpu.VMEM((n_rows, list_len), jnp.int32),
                pltpu.VMEM((n_rows, list_len), jnp.int32),
                pltpu.VMEM((1, n_rows), jnp.int32),
                lists, lists, lists,
                pltpu.VMEM((all_rows // 2, LANES), jnp.float32),
                pltpu.VMEM((groups, n_rows // 2, LANES), jnp.float32),
                pltpu.VMEM((SLOTS, TILE, width), jnp.bfloat16),
                scores, scores,
                sems((4,)), sems((SLOTS,)), sems((PIECES,)), sems((PIECES,)), sems((PIECES,)), sems((PIECES,)),
                sems((2 * groups,)), sems((2 * groups,)),
            ],
            compiler_params=pltpu.CompilerParams(vmem_limit_bytes=56 * 1024 * 1024, collective_id=0, has_side_effects=True),
            name="fused",
        )(h_loc, ids_loc, valid_loc, tgt_loc.reshape(1, n_rows), w_loc)
        return p, lp.reshape(n_rows)

    return jax.shard_map(
        local_step,
        mesh=mesh,
        in_specs=(rows_spec, P("vocab", None), rows_spec, rows_spec, vec_spec),
        out_specs=(rows_spec, vec_spec),
        check_vma=False,
    )
```

time: 58.7 us -> 57.4 us (0.978)
  local copies, waits for them, and re-layouts: 4.22 us -> 2.55 us
    unnamed x10 -> x2, local copies, waits for them, and re-layouts: 4.22 us -> 2.55 us
where the time goes in v3:
time: 57.4 us; the launch traced here: 56.9 us
  Pallas kernels  53.7 us (94%)
  local copies, waits for them, and re-layouts  2.55 us (4%)
  between operations  0.64 us (1%)
    pallas_call x1, Pallas kernels, local_step(): pl.pallas_call(functools.partial(kernel, groups // 2), out_shape=(jax.Sha...  53.7 us
    unnamed x2, local copies, waits for them, and re-layouts  2.55 us

profile of v3, /device:TPU:112, one launch (start us, length us, event | category | flops | bytes accessed | tf_op | source)
XLA Modules:
  0.0 56.9 jit_solution(7761222856137730854)
XLA Ops:
  0.6 53.7 %fused.1 = (f32[64,64]{1,0:T(8,128)}, f32[1,64]{1,0:T(1,128)}) custom-call(bf16[64,1536]{1,0:T(8,128)(2,1)} %h_hbm.1, s32[64,64]{1,0:T(8,128)} %ids_hbm.1, s32[64,64]{1,0:T(8,128)} %valid_hbm.1, s32[1,64]{1,0:T(1,128)} %bitcast.2, bf16[18992,1536]{1,0:T(8,128)(2,1)} %w_hbm.1), custom_call_target="tpu_custom_call" | custom-call | tf_op jit(solution)/shard_map/fused/pallas_call | solution.py:275
  54.4 1.4 %copy.9 = f32[64,64]{1,0:T(8,128)} copy(f32[64,64]{1,0:T(8,128)} %get-tuple-element.8) | data formatting | bytes 32768
  55.7 1.2 %copy.10 = f32[64]{0:T(128)} copy(f32[64]{0:T(128)} %bitcast.3) | data formatting | bytes 512
